TPU v7x, 32 devices: a whole 2x2x4 slice. The times are simulated.
32 devices in a mesh: lat: 4 (over y, core), lon: 4 (over z), lev: 2 (over x).
Axes of the slice: x: 2, y: 2, z: 4, core: 2. Of those that a mesh axis runs over, the one named last changes fastest.
Arguments:
- density: float32 [128, 16, 256, 128], P('lat', 'lon', 'lev'), may hold values from 0.2 to 1.8
- crowding: float32 [128, 16, 256, 128], P('lat', 'lon', 'lev'), may hold values from 0.5 to 2
Outputs:
- running_total: float32 [128, 16, 256, 128], P('lat', 'lon', 'lev')
- density_end: float32 [128, 16, 256, 128], P('lat', 'lon', 'lev')
All inputs are finite; a program needn't handle non-finite values.
Results may differ from a plain program's by a relative error of at most 0.00002.
Values sent between devices are 32-bit elements; how exact they have to be, the bound alone decides.
A program may use at most 320 MiB of HBM per device.

v0:
```python
import functools

import jax
import jax.numpy as jnp
from jax import lax
from jax.experimental import pallas as pl
from jax.experimental.pallas import tpu as pltpu
from jax.sharding import PartitionSpec as P

STEPS = 4
CHUNKS = 16
MESH = pl.DeviceIdType.MESH
LO, HI = 0, 1


def kernel(
    sizes, density, crowding, running, density_end,
    field, crowd, lon, lev,
    load_sem, crowd_sem,
    lon_send, lon_recv, lev_send, lev_recv, lat_send, lat_recv, credit,
):
    n_lat, n_lon, n_lev = sizes
    J, I, K, L = density.shape
    rows = max(1, J // CHUNKS)
    chunks = J // rows
    names = {"lat": n_lat, "lon": n_lon, "lev": n_lev}
    me = {name: lax.axis_index(name) for name in names}
    near = {
        name: (
            {name: lax.rem(me[name] + n - 1, n)},
            {name: lax.rem(me[name] + 1, n)},
        )
        for name, n in names.items()
    }

    def load(c):
        own = pl.ds(c * rows, rows)
        return pltpu.make_async_copy(density.at[own], field.at[0, pl.ds(1 + c * rows, rows)], load_sem.at[c])

    def load_crowd(c):
        own = pl.ds(c * rows, rows)
        return pltpu.make_async_copy(crowding.at[own], crowd.at[own], crowd_sem.at[c])

    def lon_copy(slot, side, c):
        plane = 0 if side == LO else I - 1
        return pltpu.make_async_remote_copy(
            src_ref=field.at[slot, pl.ds(1 + c * rows, rows), plane],
            dst_ref=lon.at[1 - side, pl.ds(c * rows, rows)],
            send_sem=lon_send.at[side, c],
            recv_sem=lon_recv.at[1 - side, c],
            device_id=near["lon"][side],
            device_id_type=MESH,
        )

    def total_copy(c):
        own = pl.ds(c * rows, rows)
        return pltpu.make_async_remote_copy(
            src_ref=running.at[own, I - 1],
            dst_ref=lon.at[LO, own],
            send_sem=lon_send.at[HI, c],
            recv_sem=lon_recv.at[LO, c],
            device_id=near["lon"][HI],
            device_id_type=MESH,
        )

    def lev_copy(slot, side, c):
        first = 0 if side == LO else K - 8
        return pltpu.make_async_remote_copy(
            src_ref=field.at[slot, pl.ds(1 + c * rows, rows), :, pl.ds(first, 8)],
            dst_ref=lev.at[slot, 1 - side, pl.ds(c * rows, rows)],
            send_sem=lev_send.at[side, c],
            recv_sem=lev_recv.at[slot, 1 - side, c],
            device_id=near["lev"][side],
            device_id_type=MESH,
        )

    def lat_copy(slot, side):
        return pltpu.make_async_remote_copy(
            src_ref=field.at[slot, 1 if side == LO else J],
            dst_ref=field.at[slot, J + 1 if side == LO else 0],
            send_sem=lat_send.at[side],
            recv_sem=lat_recv.at[slot, 1 - side],
            device_id=near["lat"][side],
            device_id_type=MESH,
        )

    def at_edges(c, act):
        @pl.when(c == 0)
        def _():
            act(LO)

        @pl.when(c == chunks - 1)
        def _():
            act(HI)

    def start_sends(slot, c):
        for side in (LO, HI):
            lon_copy(slot, side, c).start()
            lev_copy(slot, side, c).start()
        at_edges(c, lambda side: lat_copy(slot, side).start())

    def end_sends(slot, c):
        for side in (LO, HI):
            lon_copy(slot, side, c).wait_send()
            lev_copy(slot, side, c).wait_send()
        at_edges(c, lambda side: lat_copy(slot, side).wait_send())

    def end_receives(slot, c):
        for side in (LO, HI):
            lon_copy(slot, side, c).wait_recv()
            lev_copy(slot, side, c).wait_recv()
        at_edges(c, lambda side: lat_copy(slot, 1 - side).wait_recv())

    def give_credit(side, c):
        pl.semaphore_signal(
            credit.at[1 - side, c], inc=1, device_id=near["lon"][side], device_id_type=MESH
        )

    def loop(count, act):
        def lap(c, carry):
            act(c)
            return carry

        lax.fori_loop(0, count, lap, 0)

    def begin(c):
        load(c).start()

    def begin_crowd(c):
        load_crowd(c).start()

    barrier = pltpu.get_barrier_semaphore()
    for name in names:
        for side in (LO, HI):
            pl.semaphore_signal(barrier, inc=1, device_id=near[name][side], device_id_type=MESH)
    loop(chunks, begin)
    pl.semaphore_wait(barrier, 2 * len(names))

    def first(c):
        load(c).wait()
        start_sends(0, c)

    loop(chunks, first)
    loop(chunks, begin_crowd)

    at_k = lax.broadcasted_iota(jnp.int32, (K, L), 0)

    def advance(slot, j, put):
        for i in range(I):
            middle = field[slot, j + 1, i]
            below = lon[LO, j] if i == 0 else field[slot, j + 1, i - 1]
            above = lon[HI, j] if i == I - 1 else field[slot, j + 1, i + 1]
            before = jnp.where(at_k == 0, lev[slot, LO, j, i, 7:8], pltpu.roll(middle, 1, 0))
            after = jnp.where(at_k == K - 1, lev[slot, HI, j, i, 0:1], pltpu.roll(middle, K - 1, 0))
            around = (field[slot, j, i] + field[slot, j + 2, i]) + (below + above) + (before + after)
            put(j, i, middle * (0.6 - 0.2 * (middle * crowd[j, i])) + 0.1 * around)

    share = 1.0 / (I * n_lon)

    def total(j):
        so_far = jnp.where(me["lon"] > 0, lon[LO, j], 0.0)
        for i in range(I):
            so_far = so_far + density_end[j, i] * share
            running[j, i] = so_far

    def add_up(c):
        @pl.when(me["lon"] > 0)
        def _():
            total_copy(c).wait_recv()

        loop(rows, lambda r: total(c * rows + r))
        pl.semaphore_wait(credit.at[HI, c], 1)

        @pl.when(me["lon"] < n_lon - 1)
        def _():
            total_copy(c).start()

    for step in range(STEPS):
        slot = step % 2
        last = step == STEPS - 1

        def put(j, i, value):
            if last:
                density_end[j, i] = value
            else:
                field[1 - slot, j + 1, i] = value

        def march(c):
            if step == 0:
                load_crowd(c).wait()
            end_receives(slot, c)
            loop(rows, lambda r: advance(slot, c * rows + r, put))
            give_credit(LO, c)
            if not last:
                give_credit(HI, c)
            end_sends(slot, c)
            if not last:
                pl.semaphore_wait(credit.at[LO, c], 1)
                pl.semaphore_wait(credit.at[HI, c], 1)
                start_sends(1 - slot, c)

        loop(chunks, march)

    loop(chunks, add_up)

    def finish(c):
        @pl.when(me["lon"] < n_lon - 1)
        def _():
            total_copy(c).wait_send()

    loop(chunks, finish)


def body(sizes, density, crowding):
    J, I, K, L = density.shape
    chunks = J // max(1, J // CHUNKS)
    shape = pltpu.VMEM(density.shape, jnp.float32)
    dma = pltpu.SemaphoreType.DMA
    return pl.pallas_call(
        functools.partial(kernel, sizes),
        out_shape=(shape, shape),
        in_specs=[pl.BlockSpec(memory_space=pl.ANY)] * 2,
        out_specs=(pl.BlockSpec(memory_space=pltpu.VMEM),) * 2,
        scratch_shapes=[
            pltpu.VMEM((2, J + 2, I, K, L), jnp.float32),
            pltpu.VMEM((J, I, K, L), jnp.float32),
            pltpu.VMEM((2, J, K, L), jnp.float32),
            pltpu.VMEM((2, 2, J, I, 8, L), jnp.float32),
            dma((chunks,)),
            dma((chunks,)),
            dma((2, chunks)),
            dma((2, chunks)),
            dma((2, chunks)),
            dma((2, 2, chunks)),
            dma((2,)),
            dma((2, 2)),
            pltpu.SemaphoreType.REGULAR((2, chunks)),
        ],
        compiler_params=pltpu.CompilerParams(
            collective_id=0, has_side_effects=True, vmem_limit_bytes=40 * 2**20
        ),
    )(density, crowding)


def solution(mesh):
    sizes = tuple(mesh.shape[name] for name in ("lat", "lon", "lev"))
    return jax.shard_map(
        functools.partial(body, sizes),
        mesh=mesh,
        in_specs=(P("lat", "lon", "lev", None), P("lat", "lon", "lev", None)),
        out_specs=(P("lat", "lon", "lev", None), P("lat", "lon", "lev", None)),
        check_vma=False,
    )
```

profile of v0, /device:TPU:24, one launch (start us, length us, event | category | flops | bytes accessed | tf_op | source)
XLA Modules:
  0.0 432.8 jit_solution(5284405992971748774)
XLA Ops:
  0.6 425.4 %shard_map.41 = (f32[32,4,128,128]{3,2,1,0:T(8,128)S(1)}, f32[32,4,128,128]{3,2,1,0:T(8,128)S(1)}) custom-call(f32[32,4,128,128]{3,2,1,0:T(8,128)} %density.1, f32[32,4,128,128]{3,2,1,0:T(8,128)} %crowding.1), custom_call_target="tpu_custom_call" | custom-call | tf_op jit(solution)/shard_map/pallas_call | solution.py:219
  426.0 3.4 copy.6
  429.4 3.4 copy.7
where the time goes:
time: 433 us
  Pallas kernels  425 us (98%)
  local copies, waits for them, and re-layouts  6.8 us (2%)
    pallas_call x1, Pallas kernels, body(): pl.pallas_call(functools.partial(kernel, sizes), out_shape=(shape, shape)...  425 us

commit v1 on v0

v1 whole, which is shorter than its diff:
```python
import functools

import jax
import jax.numpy as jnp
from jax import lax
from jax.experimental import pallas as pl
from jax.experimental.pallas import tpu as pltpu
from jax.sharding import PartitionSpec as P

STEPS = 4
CHUNKS = 16
LEAD = 6
EXTRA = 4
PART = 1
MESH = pl.DeviceIdType.MESH
LO, HI = 0, 1


def loop(count, act):
    def lap(c, carry):
        act(c)
        return carry

    lax.fori_loop(0, count, lap, 0)


def kernel(
    sizes, density, crowding, running, density_end,
    field, crowd, lon, below, lev,
    load_sem, crowd_sem,
    lon_send, lon_recv, lev_send, lev_recv, lat_send, lat_recv, total_send, total_recv, credit,
):
    n_lat, n_lon, n_lev = sizes
    J, I, K, L = density.shape
    rows = max(1, J // CHUNKS)
    chunks = J // rows
    names = {"lat": n_lat, "lon": n_lon, "lev": n_lev}
    me = {name: lax.axis_index(name) for name in names}
    near = {
        name: (
            {name: lax.rem(me[name] + n - 1, n)},
            {name: lax.rem(me[name] + 1, n)},
        )
        for name, n in names.items()
    }

    def load(c):
        own = pl.ds(c * rows, rows)
        return pltpu.make_async_copy(density.at[own], field.at[0, pl.ds(1 + c * rows, rows)], load_sem.at[c])

    def load_crowd():
        return pltpu.make_async_copy(crowding, crowd, crowd_sem)

    def remote(src, dst, send_sem, recv_sem, name, side):
        return pltpu.make_async_remote_copy(
            src_ref=src,
            dst_ref=dst,
            send_sem=send_sem,
            recv_sem=recv_sem,
            device_id=near[name][side],
            device_id_type=MESH,
        )

    def lon_copy(slot, side, c):
        own = pl.ds(c * rows, rows)
        plane = 0 if side == LO else I - 1
        return remote(
            field.at[slot, pl.ds(1 + c * rows, rows), plane], lon.at[1 - side, own],
            lon_send.at[slot], lon_recv.at[c], "lon", side,
        )

    def lon_both(slot, c):
        own = lon.at[:, pl.ds(c * rows, rows)]
        return remote(own, own, lon_send.at[slot], lon_recv.at[c], "lon", HI)

    def lon_all(slot):
        return remote(lon, lon, lon_send.at[slot], lon_recv.at[0], "lon", HI)

    def total_copy(p):
        own = pl.ds(p * PART, PART)
        return remote(
            running.at[own, I - 1], below.at[own], total_send, total_recv.at[p], "lon", HI
        )

    def total_all():
        return remote(below, below, total_send, total_recv.at[0], "lon", HI)

    def lev_copy(slot, side, c):
        own = pl.ds(c * rows, rows)
        first = 0 if side == LO else K - 8
        return remote(
            field.at[slot, pl.ds(1 + c * rows, rows), :, pl.ds(first, 8)], lev.at[slot, 1 - side, own],
            lev_send.at[slot], lev_recv.at[slot, c], "lev", side,
        )

    def lev_both(slot, c):
        own = lev.at[slot, :, pl.ds(c * rows, rows)]
        return remote(own, own, lev_send.at[slot], lev_recv.at[slot, c], "lev", HI)

    def lev_all(slot):
        return remote(lev.at[slot], lev.at[slot], lev_send.at[slot], lev_recv.at[slot, 0], "lev", HI)

    def lat_copy(slot, side):
        return remote(
            field.at[slot, 1 if side == LO else J], field.at[slot, J + 1 if side == LO else 0],
            lat_send.at[side], lat_recv.at[slot, 1 - side], "lat", side,
        )

    def at_edges(c, act):
        @pl.when(c == 0)
        def _():
            act(LO)

        @pl.when(c == chunks - 1)
        def _():
            act(HI)

    def start_sides(slot, c):
        for side in (LO, HI):
            lev_copy(slot, side, c).start()
        at_edges(c, lambda side: lat_copy(slot, side).start())

    def end_receives(slot, c):
        lon_both(slot, c).wait_recv()
        lev_both(slot, c).wait_recv()
        at_edges(c, lambda side: lat_copy(slot, 1 - side).wait_recv())

    def trade_credit(c):
        for side in (LO, HI):
            pl.semaphore_signal(credit.at[c], inc=1, device_id=near["lon"][side], device_id_type=MESH)
        pl.semaphore_wait(credit.at[c], 2)

    barrier = pltpu.get_barrier_semaphore()
    for name in names:
        for side in (LO, HI):
            pl.semaphore_signal(barrier, inc=1, device_id=near[name][side], device_id_type=MESH)
    loop(chunks, lambda c: load(c).start())
    pl.semaphore_wait(barrier, 2 * len(names))

    def first(c):
        load(c).wait()
        for side in (LO, HI):
            lon_copy(0, side, c).start()
        start_sides(0, c)

    loop(chunks, first)
    load_crowd().start()

    at_k = lax.broadcasted_iota(jnp.int32, (K, L), 0)

    def advance(slot, j, put):
        for i in range(I):
            middle = field[slot, j + 1, i]
            lower = lon[LO, j] if i == 0 else field[slot, j + 1, i - 1]
            upper = lon[HI, j] if i == I - 1 else field[slot, j + 1, i + 1]
            before = jnp.where(at_k == 0, lev[slot, LO, j, i, 7:8], pltpu.roll(middle, 1, 0))
            after = jnp.where(at_k == K - 1, lev[slot, HI, j, i, 0:1], pltpu.roll(middle, K - 1, 0))
            around = (field[slot, j, i] + field[slot, j + 2, i]) + (lower + upper) + (before + after)
            put(j, i, middle * (0.6 - 0.2 * (middle * crowd[j, i])) + 0.1 * around)

    share = 1.0 / (I * n_lon)
    start = me["lon"] == 0
    end = me["lon"] == n_lon - 1
    lead = jnp.where(end, chunks, jnp.minimum(LEAD + EXTRA * me["lon"], chunks))

    def total(j):
        so_far = jnp.where(me["lon"] > 0, below[j], 0.0)
        for i in range(I):
            so_far = so_far + density_end[j, i] * share
            running[j, i] = so_far

    def put_field(slot):
        def put(j, i, value):
            field[slot, j + 1, i] = value

        return put

    def put_end(j, i, value):
        density_end[j, i] = value

    def march(step, c):
        slot = step % 2
        end_receives(slot, c)
        loop(rows, lambda r: advance(slot, c * rows + r, put_field(1 - slot)))
        at_edges(c, lambda side: lat_copy(slot, side).wait_send())
        start_sides(1 - slot, c)
        trade_credit(c)
        if step < STEPS - 2:
            for side in (LO, HI):
                lon_copy(1 - slot, side, c).start()
            return

        @pl.when(jnp.logical_not(start))
        def _():
            lon_copy(1 - slot, LO, c).start()

        @pl.when(c >= chunks - lead)
        def _():
            lon_copy(1 - slot, HI, c - (chunks - lead)).start()

    def march_last(c):
        slot = (STEPS - 1) % 2
        end_receives(slot, c)
        loop(rows, lambda r: advance(slot, c * rows + r, put_end))

        @pl.when(c < chunks - lead)
        def _():
            lon_copy(slot, HI, c + lead).start()

        def add_up(r):
            p = c * (rows // PART) + r

            @pl.when(jnp.logical_not(start))
            def _():
                total_copy(p).wait_recv()

            for q in range(PART):
                total(p * PART + q)

            @pl.when(jnp.logical_not(end))
            def _():
                total_copy(p).start()

        loop(rows // PART, add_up)

        @pl.when(start)
        def _():
            lon_copy(slot, LO, c).start()

    load_crowd().wait()
    for step in range(STEPS - 1):
        loop(chunks, lambda c: march(step, c))
        lon_all(step % 2).wait_send()
        lev_all(step % 2).wait_send()
    loop(chunks, march_last)
    slot = (STEPS - 1) % 2
    lon_all(slot).wait_send()
    lev_all(slot).wait_send()
    for side in (LO, HI):
        lat_copy(slot, side).wait_send()

    @pl.when(jnp.logical_not(end))
    def _():
        total_all().wait_send()


def body(sizes, density, crowding):
    J, I, K, L = density.shape
    chunks = J // max(1, J // CHUNKS)
    shape = pltpu.VMEM(density.shape, jnp.float32)
    dma = pltpu.SemaphoreType.DMA
    return pl.pallas_call(
        functools.partial(kernel, sizes),
        out_shape=(shape, shape),
        in_specs=[pl.BlockSpec(memory_space=pl.ANY)] * 2,
        out_specs=(pl.BlockSpec(memory_space=pltpu.VMEM),) * 2,
        scratch_shapes=[
            pltpu.VMEM((2, J + 2, I, K, L), jnp.float32),
            pltpu.VMEM((J, I, K, L), jnp.float32),
            pltpu.VMEM((2, J, K, L), jnp.float32),
            pltpu.VMEM((J, K, L), jnp.float32),
            pltpu.VMEM((2, 2, J, I, 8, L), jnp.float32),
            dma((chunks,)),
            dma,
            dma((2,)),
            dma((chunks,)),
            dma((2,)),
            dma((2, chunks)),
            dma((2,)),
            dma((2, 2)),
            dma,
            dma((J // PART,)),
            pltpu.SemaphoreType.REGULAR((chunks,)),
        ],
        compiler_params=pltpu.CompilerParams(
            collective_id=0, has_side_effects=True, vmem_limit_bytes=42 * 2**20
        ),
    )(density, crowding)


def solution(mesh):
    sizes = tuple(mesh.shape[name] for name in ("lat", "lon", "lev"))
    return jax.shard_map(
        functools.partial(body, sizes),
        mesh=mesh,
        in_specs=(P("lat", "lon", "lev", None), P("lat", "lon", "lev", None)),
        out_specs=(P("lat", "lon", "lev", None), P("lat", "lon", "lev", None)),
        check_vma=False,
    )
```

time: 433 us -> 422 us (0.975)
  Pallas kernels: 425 us -> 415 us
    pallas_call x1, Pallas kernels: 425 us -> 415 us  [body(): pl.pallas_call(functools.partial(kernel, sizes), out_shape=(shape, shape)...]
where the time goes in v1:
time: 422 us
  Pallas kernels  415 us (98%)
  local copies, waits for them, and re-layouts  6.8 us (2%)
    pallas_call x1, Pallas kernels, body(): pl.pallas_call(functools.partial(kernel, sizes), out_shape=(shape, shape)...  415 us

profile of v1, /device:TPU:24, one launch (start us, length us, event | category | flops | bytes accessed | tf_op | source)
XLA Modules:
  0.0 422.0 jit_solution(6743755782697512586)
XLA Ops:
  0.6 414.6 %shard_map.41 = (f32[32,4,128,128]{3,2,1,0:T(8,128)S(1)}, f32[32,4,128,128]{3,2,1,0:T(8,128)S(1)}) custom-call(f32[32,4,128,128]{3,2,1,0:T(8,128)} %density.1, f32[32,4,128,128]{3,2,1,0:T(8,128)} %crowding.1), custom_call_target="tpu_custom_call" | custom-call | tf_op jit(solution)/shard_map/pallas_call | solution.py:252
  415.2 3.4 copy.6
  418.6 3.4 copy.7

commit v2 on v1

v2 whole, which is shorter than its diff:
```python
import functools

import jax
import jax.numpy as jnp
from jax import lax
from jax.experimental import pallas as pl
from jax.experimental.pallas import tpu as pltpu
from jax.sharding import PartitionSpec as P

STEPS = 4
BULK = 16
FINE = 32
LEAD = 12
EXTRA = 8
PIECES = 4
LOADS = 8
EDGES = 4
STORES = 8
MESH = pl.DeviceIdType.MESH
LO, HI = 0, 1


def cut(length, count):
    size = max(1, length // count)
    return size, length // size


def loop(count, act):
    def lap(c, carry):
        act(c)
        return carry

    lax.fori_loop(0, count, lap, 0)


def kernel(
    sizes, density, crowding, carry, density_end,
    field, crowd, lon, below, totals, lev,
    load_sem, crowd_sem, lon_send, lon_recv, lev_send, lev_recv,
    lat_send, lat_recv, total_send, total_recv, piece_recv, credit,
):
    n_lat, n_lon, n_lev = sizes
    J, I, K, L = density.shape
    rows, chunks = cut(J, BULK)
    some, parts = cut(rows, max(1, FINE // chunks))
    fine = chunks * parts
    batch, batches = cut(chunks, LOADS)
    span, spans = cut(chunks, EDGES)
    names = {"lat": n_lat, "lon": n_lon, "lev": n_lev}
    me = {name: lax.axis_index(name) for name in names}
    near = {
        name: (
            {name: lax.rem(me[name] + n - 1, n)},
            {name: lax.rem(me[name] + 1, n)},
        )
        for name, n in names.items()
    }

    def load(c):
        first, count = c * batch * rows, batch * rows
        return pltpu.make_async_copy(
            density.at[pl.ds(first, count)], field.at[0, pl.ds(1 + first, count)], load_sem.at[c]
        )

    def load_crowd():
        return pltpu.make_async_copy(crowding, crowd, crowd_sem)

    def remote(src, dst, send_sem, recv_sem, name, side):
        return pltpu.make_async_remote_copy(
            src_ref=src,
            dst_ref=dst,
            send_sem=send_sem,
            recv_sem=recv_sem,
            device_id=near[name][side],
            device_id_type=MESH,
        )

    def lon_copy(slot, side, first, count, recv_sem):
        plane = 0 if side == LO else I - 1
        return remote(
            field.at[slot, pl.ds(1 + first, count), plane], lon.at[1 - side, pl.ds(first, count)],
            lon_send.at[slot], recv_sem, "lon", side,
        )

    def lon_bulk(slot, side, c):
        return lon_copy(slot, side, c * rows, rows, lon_recv.at[c * parts])

    def lon_fine(side, f):
        return lon_copy((STEPS - 1) % 2, side, f * some, some, lon_recv.at[f])

    def lon_both(first, count, recv_sem):
        own = lon.at[:, pl.ds(first, count)]
        return remote(own, own, lon_send.at[0], recv_sem, "lon", HI)

    def lon_all(slot):
        return remote(lon, lon, lon_send.at[slot], lon_recv.at[0], "lon", HI)

    def total_copy(f):
        own = pl.ds(f * some, some)
        return remote(totals.at[own], below.at[own], total_send, total_recv.at[f], "lon", HI)

    def piece_copy(j, p):
        own = pl.ds(p * (K // PIECES), K // PIECES)
        return remote(
            totals.at[j, own], below.at[j, own], total_send, piece_recv.at[j - (J - some), p], "lon", HI
        )

    def total_all():
        return remote(below, below, total_send, total_recv.at[0], "lon", HI)

    def lev_copy(slot, side, g):
        start, count = g * span * rows, span * rows
        first = 0 if side == LO else K - 8
        return remote(
            field.at[slot, pl.ds(1 + start, count), :, pl.ds(first, 8)],
            lev.at[slot, 1 - side, pl.ds(start, count)],
            lev_send.at[slot], lev_recv.at[slot, g], "lev", side,
        )

    def lev_both(slot, g):
        own = lev.at[slot, :, pl.ds(g * span * rows, span * rows)]
        return remote(own, own, lev_send.at[slot], lev_recv.at[slot, g], "lev", HI)

    def lev_all(slot):
        return remote(lev.at[slot], lev.at[slot], lev_send.at[slot], lev_recv.at[slot, 0], "lev", HI)

    def lat_copy(slot, side):
        return remote(
            field.at[slot, 1 if side == LO else J], field.at[slot, J + 1 if side == LO else 0],
            lat_send.at[side], lat_recv.at[slot, 1 - side], "lat", side,
        )

    def at_edges(c, act):
        @pl.when(c == 0)
        def _():
            act(LO)

        @pl.when(c == chunks - 1)
        def _():
            act(HI)

    def start_sides(slot, c):
        @pl.when(lax.rem(c, span) == span - 1)
        def _():
            for side in (LO, HI):
                lev_copy(slot, side, lax.div(c, span)).start()

        at_edges(c, lambda side: lat_copy(slot, side).start())

    def end_receives(slot, c):
        @pl.when(lax.rem(c, span) == 0)
        def _():
            lev_both(slot, lax.div(c, span)).wait_recv()

        at_edges(c, lambda side: lat_copy(slot, 1 - side).wait_recv())

    def trade_credit(c):
        for side in (LO, HI):
            pl.semaphore_signal(credit.at[c], inc=1, device_id=near["lon"][side], device_id_type=MESH)
        pl.semaphore_wait(credit.at[c], 2)

    barrier = pltpu.get_barrier_semaphore()
    for name in names:
        for side in (LO, HI):
            pl.semaphore_signal(barrier, inc=1, device_id=near[name][side], device_id_type=MESH)
    loop(batches, lambda c: load(c).start())
    pl.semaphore_wait(barrier, 2 * len(names))

    def first(c):
        @pl.when(lax.rem(c, batch) == 0)
        def _():
            load(lax.div(c, batch)).wait()

        for side in (LO, HI):
            lon_bulk(0, side, c).start()
        start_sides(0, c)

    loop(chunks, first)
    load_crowd().start()

    at_k = lax.broadcasted_iota(jnp.int32, (K, L), 0)

    def advance(slot, j, put):
        for i in range(I):
            middle = field[slot, j + 1, i]
            lower = lon[LO, j] if i == 0 else field[slot, j + 1, i - 1]
            upper = lon[HI, j] if i == I - 1 else field[slot, j + 1, i + 1]
            before = jnp.where(at_k == 0, lev[slot, LO, j, i, 7:8], pltpu.roll(middle, 1, 0))
            after = jnp.where(at_k == K - 1, lev[slot, HI, j, i, 0:1], pltpu.roll(middle, K - 1, 0))
            around = (field[slot, j, i] + field[slot, j + 2, i]) + (lower + upper) + (before + after)
            put(j, i, middle * (0.6 - 0.2 * (middle * crowd[j, i])) + 0.1 * around)

    share = 1.0 / (I * n_lon)
    start = me["lon"] == 0
    end = me["lon"] == n_lon - 1
    lead = jnp.where(end, fine, jnp.minimum(LEAD + EXTRA * me["lon"], fine))

    def add_up(j, own):
        so_far = jnp.where(me["lon"] > 0, below[j, own], 0.0)
        carry[j, own] = so_far
        for i in range(I):
            so_far = so_far + density_end[j, i, own] * share
        totals[j, own] = so_far

    def pass_on(copy, act):
        @pl.when(jnp.logical_not(start))
        def _():
            copy.wait_recv()

        act()

        @pl.when(jnp.logical_not(end))
        def _():
            copy.start()

    def put_field(slot):
        def put(j, i, value):
            field[slot, j + 1, i] = value

        return put

    def put_end(j, i, value):
        density_end[j, i] = value

    def march(step, c):
        slot = step % 2
        lon_both(c * rows, rows, lon_recv.at[c * parts]).wait_recv()
        end_receives(slot, c)
        loop(rows, lambda r: advance(slot, c * rows + r, put_field(1 - slot)))
        at_edges(c, lambda side: lat_copy(slot, side).wait_send())
        start_sides(1 - slot, c)
        trade_credit(c)
        if step < STEPS - 2:
            for side in (LO, HI):
                lon_bulk(1 - slot, side, c).start()
            return

        def send(r):
            f = c * parts + r

            @pl.when(jnp.logical_not(start))
            def _():
                lon_fine(LO, f).start()

            @pl.when(f >= fine - lead)
            def _():
                lon_fine(HI, f - (fine - lead)).start()

        loop(parts, send)

    def march_last(c, r):
        slot = (STEPS - 1) % 2
        f = c * parts + r
        lon_both(f * some, some, lon_recv.at[f]).wait_recv()
        loop(some, lambda q: advance(slot, f * some + q, put_end))

        @pl.when(f < fine - lead)
        def _():
            lon_fine(HI, f + lead).start()

        @pl.when(f < fine - 1)
        def _():
            pass_on(total_copy(f), lambda: loop(some, lambda q: add_up(f * some + q, slice(None))))

        @pl.when(f == fine - 1)
        def _():
            for j in range(J - some, J):
                for p in range(PIECES):
                    size = K // PIECES
                    pass_on(piece_copy(j, p), lambda: add_up(j, slice(p * size, (p + 1) * size)))

        @pl.when(start)
        def _():
            lon_fine(LO, f).start()

    def march_end(c):
        end_receives((STEPS - 1) % 2, c)
        loop(parts, lambda r: march_last(c, r))

    load_crowd().wait()
    for step in range(STEPS - 1):
        loop(chunks, lambda c: march(step, c))
        lon_all(step % 2).wait_send()
        lev_all(step % 2).wait_send()
    loop(chunks, march_end)
    slot = (STEPS - 1) % 2
    lon_all(slot).wait_send()
    lev_all(slot).wait_send()
    for side in (LO, HI):
        lat_copy(slot, side).wait_send()

    @pl.when(jnp.logical_not(end))
    def _():
        total_all().wait_send()


def store(size, density_end, carry, running, end, sums, sems):
    J, I, K, L = density_end.shape
    rows, chunks = cut(J, STORES)
    share = 1.0 / size

    def end_copy(own):
        return pltpu.make_async_copy(density_end.at[own], end.at[own], sems.at[0])

    def running_copy(own):
        return pltpu.make_async_copy(sums.at[own], running.at[own], sems.at[1])

    loop(chunks, lambda c: end_copy(pl.ds(c * rows, rows)).start())

    def add_up(j):
        so_far = carry[j]
        for i in range(I):
            so_far = so_far + density_end[j, i] * share
            sums[j, i] = so_far

    def some(c):
        loop(rows, lambda r: add_up(c * rows + r))
        running_copy(pl.ds(c * rows, rows)).start()

    loop(chunks, some)
    end_copy(pl.ds(0, J)).wait()
    running_copy(pl.ds(0, J)).wait()


def body(sizes, density, crowding):
    J, I, K, L = density.shape
    rows, chunks = cut(J, BULK)
    some, parts = cut(rows, max(1, FINE // chunks))
    fine = chunks * parts
    batches, spans = cut(chunks, LOADS)[1], cut(chunks, EDGES)[1]
    dma = pltpu.SemaphoreType.DMA
    whole = jax.ShapeDtypeStruct(density.shape, jnp.float32)
    vmem = pl.BlockSpec(memory_space=pltpu.VMEM)
    hbm = pl.BlockSpec(memory_space=pl.ANY)
    carry, density_end = pl.pallas_call(
        functools.partial(kernel, sizes),
        out_shape=(pltpu.VMEM((J, K, L), jnp.float32), pltpu.VMEM(density.shape, jnp.float32)),
        in_specs=[hbm] * 2,
        out_specs=(vmem,) * 2,
        scratch_shapes=[
            pltpu.VMEM((2, J + 2, I, K, L), jnp.float32),
            pltpu.VMEM((J, I, K, L), jnp.float32),
            pltpu.VMEM((2, J, K, L), jnp.float32),
            pltpu.VMEM((J, K, L), jnp.float32),
            pltpu.VMEM((J, K, L), jnp.float32),
            pltpu.VMEM((2, 2, J, I, 8, L), jnp.float32),
            dma((batches,)),
            dma,
            dma((2,)),
            dma((fine,)),
            dma((2,)),
            dma((2, spans)),
            dma((2,)),
            dma((2, 2)),
            dma,
            dma((fine,)),
            dma((some, PIECES)),
            pltpu.SemaphoreType.REGULAR((chunks,)),
        ],
        compiler_params=pltpu.CompilerParams(
            collective_id=0, has_side_effects=True, vmem_limit_bytes=40 * 2**20
        ),
    )(density, crowding)
    return pl.pallas_call(
        functools.partial(store, I * sizes[1]),
        out_shape=(whole, whole),
        in_specs=[vmem] * 2,
        out_specs=(hbm,) * 2,
        scratch_shapes=[pltpu.VMEM(density.shape, jnp.float32), dma((2,))],
        compiler_params=pltpu.CompilerParams(vmem_limit_bytes=10 * 2**20),
    )(density_end, carry)


def solution(mesh):
    sizes = tuple(mesh.shape[name] for name in ("lat", "lon", "lev"))
    return jax.shard_map(
        functools.partial(body, sizes),
        mesh=mesh,
        in_specs=(P("lat", "lon", "lev", None), P("lat", "lon", "lev", None)),
        out_specs=(P("lat", "lon", "lev", None), P("lat", "lon", "lev", None)),
        check_vma=False,
    )
```

time: 422 us -> 421 us (level)
  local copies, waits for them, and re-layouts: 6.8 us -> 0 us
  Pallas kernels: 415 us -> 420 us
    unnamed x2 -> x0, local copies, waits for them, and re-layouts: 6.8 us -> none
    pallas_call x1 -> x2, Pallas kernels: 415 us -> 420 us  [the longest x1 414 us: body(): pl.pallas_call(functools.partial(kernel, sizes), out_shape=(pltpu.VMEM((J...]
where the time goes in v2:
time: 421 us
  Pallas kernels  420 us (100%)
    pallas_call x1, Pallas kernels, body(): pl.pallas_call(functools.partial(kernel, sizes), out_shape=(pltpu.VMEM((J...  414 us

profile of v2, /device:TPU:24, one launch (start us, length us, event | category | flops | bytes accessed | tf_op | source)
XLA Modules:
  0.0 420.8 jit_solution(9664400160798190244)
XLA Ops:
  0.6 414.3 %shard_map.41 = (f32[32,128,128]{2,1,0:T(8,128)S(1)}, f32[32,4,128,128]{3,2,1,0:T(8,128)S(1)}) custom-call(f32[32,4,128,128]{3,2,1,0:T(8,128)} %density.1, f32[32,4,128,128]{3,2,1,0:T(8,128)} %crowding.1), custom_call_target="tpu_custom_call" | custom-call | tf_op jit(solution)/shard_map/pallas_call | solution.py:335
  414.9 5.8 %shard_map.42 = (f32[32,4,128,128]{3,2,1,0:T(8,128)}, f32[32,4,128,128]{3,2,1,0:T(8,128)}) custom-call(f32[32,4,128,128]{3,2,1,0:T(8,128)S(1)} %get-tuple-element.4.density_end, f32[32,128,128]{2,1,0:T(8,128)S(1)} %get-tuple-element.5.carry), custom_call_target="tpu_custom_call" | custom-call | tf_op jit(solution)/shard_map/pallas_call | solution.py:364
